TPU v7x, 16 devices: a 4x2x1 block of a 4x4x8 slice. The times are simulated.
16 devices in a mesh: dp: 4 (over y, z, core), tp: 4 (over x).
Axes of the slice: x: 4, y: 2, z: 1, core: 2. Of those that a mesh axis runs over, the one named last changes fastest.
The devices are a block of a 4x4x8 slice.
Arguments:
- x: bfloat16 [8192, 2048], P('dp'), parts along dimension 0
- dy: bfloat16 [8192, 2048], P('dp'), parts along dimension 0
- gate: bfloat16 [8192, 5120], P('dp', 'tp'), parts along dimension 0
- up: bfloat16 [8192, 5120], P('dp', 'tp'), parts along dimension 0
- w_gate: bfloat16 [2048, 5120], P(None, 'tp')
- w_up: bfloat16 [2048, 5120], P(None, 'tp')
- w_down: bfloat16 [5120, 2048], P('tp')
Outputs:
- output 1: bfloat16 [8192, 2048], P('dp'), parts along dimension 0
- output 2: bfloat16 [8192, 5120], P('dp', 'tp'), parts along dimension 0
- output 3: bfloat16 [8192, 5120], P('dp', 'tp'), parts along dimension 0
- output 4: bfloat16 [20480, 2048], P(('dp', 'tp')), parts along dimension 0
There are 4 independent parts. A program takes and returns all parts, laid end to end along the dimension named above; an argument that names none is the same for every part.
All inputs are finite; a program needn't handle non-finite values.
Results may differ from a plain program's by a relative error of at most 0.012.
Values are sent between devices in bfloat16 or wider.
A program may use at most 768 MiB of HBM per device.

v0:
```python
import functools
import math

import jax
import jax.numpy as jnp
from jax import lax
from jax.experimental import pallas as pl
from jax.experimental.pallas import tpu as pltpu
from jax.sharding import PartitionSpec as P

MESH = pl.DeviceIdType.MESH
ANY = pl.BlockSpec(memory_space=pl.ANY)
BF16, F32 = jnp.bfloat16, jnp.float32
C = math.sqrt(2.0 / math.pi)
BLK = 256
NT = 256
XT = 256


def dot(a, b, ca, cb):
    return lax.dot_general(a, b, (((ca,), (cb,)), ((), ())), preferred_element_type=F32)


def ring_kernel(
    x, dy, gate, up, w_gate, w_up, w_down,
    own_a, own_b, r_a, r_b, l_a, l_b, hid, dw_gate, dw_up,
    wg, wu, wd, dg, du, dyb, gb, ub, hidb, snd, rcv, own, xb, og, ou,
    wd_sem, w_sem, blk_sem, hid_sem, ssem, rsem, ag_ssem, ag_rsem, own_sem, x_sem, o_sem,
):
    me = lax.axis_index("tp")
    right, left = lax.rem(me + 1, 4), lax.rem(me + 3, 4)
    rows, width = dy.shape
    ff = gate.shape[1]
    chunk, half = rows // 4, width // 2

    order = ((2, 0), (2, 1), (3, 0), (1, 0), (3, 1), (1, 1), (0, 0), (0, 1))

    def start_row(j):
        k, b = order[j]
        return pl.multiple_of(lax.rem(me + k, 4) * chunk + b * BLK, BLK)

    def block_copies(j):
        s, r = j % 2, pl.ds(start_row(j), BLK)
        return (
            pltpu.make_async_copy(dy.at[r], dyb.at[s], blk_sem.at[s, 0]),
            pltpu.make_async_copy(gate.at[r], gb.at[s], blk_sem.at[s, 1]),
            pltpu.make_async_copy(up.at[r], ub.at[s], blk_sem.at[s, 2]),
        )

    def wd_copy(n):
        r = pl.ds(n * NT, NT)
        return pltpu.make_async_copy(w_down.at[r], wd.at[r], wd_sem.at[n])

    def w_copy(i, h):
        r = pl.ds(h * half, half)
        return pltpu.make_async_copy((w_gate, w_up)[i].at[r], (wg, wu)[i].at[r], w_sem.at[i, h])

    nt = ff // NT
    first = block_copies(0)
    first[0].start()
    wd_copy(0).start()
    first[1].start()
    first[2].start()
    for n in range(1, nt):
        wd_copy(n).start()
    for h in range(2):
        for i in range(2):
            w_copy(i, h).start()
    for c in block_copies(1):
        c.start()

    barrier = pltpu.get_barrier_semaphore()
    for d in (left, right):
        pl.semaphore_signal(barrier, inc=1, device_id={"tp": d}, device_id_type=MESH)

    def hid_copy(j):
        return pltpu.make_async_copy(hidb.at[j % 2], hid.at[pl.ds(start_row(j), BLK)], hid_sem.at[j % 2])

    def hidden(j):
        s, r0 = j % 2, start_row(j)
        for c in block_copies(j):
            c.wait()
        if j >= 2:
            hid_copy(j - 2).wait()

        def tile(n):
            cols = pl.ds(pl.multiple_of(n * NT, NT), NT)
            dh = dot(dyb[s], wd[cols, :], 1, 1)
            g = gb[s, :, cols].astype(F32)
            u = ub[s, :, cols].astype(F32)
            g2 = g * g
            t = jnp.tanh(C * (g + 0.044715 * (g * g2)))
            cdf = 0.5 * (1.0 + t)
            act = g * cdf
            hidb[s, :, cols] = (act * u).astype(BF16)
            du[pl.ds(r0, BLK), cols] = (dh * act).astype(BF16)
            slope = cdf + (0.5 * C) * g * (1.0 - t * t) * (1.0 + (3 * 0.044715) * g2)
            dg[pl.ds(r0, BLK), cols] = (dh * u * slope).astype(BF16)

        if j == 0:
            for n in range(nt):
                wd_copy(n).wait()
                tile(n)
        else:
            pl.loop(0, nt)(tile)
        if j + 2 < len(order):
            for c in block_copies(j + 2):
                c.start()
        hid_copy(j).start()

    def term(j, h, adds, dst, row):
        r = pl.ds(start_row(j), BLK)
        if j == 0:
            w_copy(0, h).wait()
            w_copy(1, h).wait()

        @pl.loop(0, half // 512)
        def _(i):
            wr = pl.ds(pl.multiple_of(h * half + i * 512, 512), 512)
            cols = pl.ds(pl.multiple_of(i * 512, 512), 512)
            t = dot(dg[r, :], wg[wr, :], 1, 1) + dot(du[r, :], wu[wr, :], 1, 1)
            for a in adds:
                t = t + rcv[a, :, cols].astype(F32)
            dst[row : row + BLK, cols] = t.astype(BF16)

    def slot(kind, b):
        return kind * 2 + b

    def reduce_copy(kind, b):
        s = slot(kind, b)
        return pltpu.make_async_remote_copy(
            src_ref=snd.at[s], dst_ref=rcv.at[s], send_sem=ssem.at[s], recv_sem=rsem.at[s],
            device_id={"tp": left if kind < 3 else right}, device_id_type=MESH,
        )

    def send(j, h, kind, adds=()):
        b = order[j][1]
        term(j, h, adds, snd.at[slot(kind, b)], 0)
        reduce_copy(kind, b).start()

    hidden(0)
    term(0, 0, (), snd.at[slot(0, 0)], 0)
    pl.semaphore_wait(barrier, 2)
    reduce_copy(0, 0).start()
    send(0, 1, 3)
    hidden(1)
    send(1, 0, 0)
    send(1, 1, 3)
    for j, h, kind in ((2, 1, 1), (3, 0, 4), (4, 1, 1), (5, 0, 4)):
        hidden(j)
        send(j, h, kind)
    for b in range(2):
        reduce_copy(0, b).wait_recv()
        send(2 + 2 * b, 0, 2, (slot(0, b),))
        reduce_copy(3, b).wait_recv()
        send(3 + 2 * b, 1, 5, (slot(3, b),))
    hidden(6)
    hidden(7)

    steps = width // XT

    def x_copy(i, s):
        return pltpu.make_async_copy(x.at[:, pl.ds(pl.multiple_of(i * XT, XT), XT)], xb.at[s], x_sem.at[s])

    def o_copies(i, s):
        r = pl.ds(pl.multiple_of(i * XT, XT), XT)
        return (
            pltpu.make_async_copy(og.at[s], dw_gate.at[r], o_sem.at[s, 0]),
            pltpu.make_async_copy(ou.at[s], dw_up.at[r], o_sem.at[s, 1]),
        )

    def weights(lo, hi):
        x_copy(lo, 0).start()
        x_copy(lo + 1, 1).start()

        @pl.loop(0, (hi - lo) // 2)
        def _(p):
            for s in range(2):
                i = lo + 2 * p + s
                x_copy(i, s).wait()

                @pl.when(p > 0)
                def _():
                    for c in o_copies(i, s):
                        c.wait()

                og[s] = dot(xb[s], dg[...], 0, 0).astype(BF16)
                ou[s] = dot(xb[s], du[...], 0, 0).astype(BF16)

                @pl.when(i + 2 < hi)
                def _():
                    x_copy(i + 2, s).start()

                for c in o_copies(i, s):
                    c.start()

        for s in range(2):
            for c in o_copies(hi - 2 + s, s):
                c.wait()

    def gather_copies(b):
        r = pl.ds(b * BLK, BLK)
        for d, h, dst in ((left, 0, r_a), (right, 1, l_b), (left, 1, r_b), (right, 0, l_a)):
            i = b * 4 + (0 if d is left else 2) + h
            yield pltpu.make_async_remote_copy(
                src_ref=own.at[h, r], dst_ref=dst.at[r], send_sem=ag_ssem.at[i], recv_sem=ag_rsem.at[i],
                device_id={"tp": d}, device_id_type=MESH,
            )

    def own_copies(b):
        r = pl.ds(b * BLK, BLK)
        return (
            pltpu.make_async_copy(own.at[0, r], own_a.at[r], own_sem.at[b, 0]),
            pltpu.make_async_copy(own.at[1, r], own_b.at[r], own_sem.at[b, 1]),
        )

    def finish(b):
        reduce_copy(4, b).wait_recv()
        reduce_copy(2, b).wait_recv()
        term(6 + b, 0, (slot(2, b), slot(4, b)), own.at[0], b * BLK)
        reduce_copy(1, b).wait_recv()
        reduce_copy(5, b).wait_recv()
        term(6 + b, 1, (slot(5, b), slot(1, b)), own.at[1], b * BLK)
        for c in gather_copies(b):
            c.start()
        for c in own_copies(b):
            c.start()

    weights(0, steps // 2)
    finish(0)
    finish(1)
    weights(steps // 2, steps)

    for kind in range(6):
        for b in range(2):
            reduce_copy(kind, b).wait_send()
    for b in range(2):
        for c in gather_copies(b):
            c.wait()
        for c in own_copies(b):
            c.wait()
    hid_copy(6).wait()
    hid_copy(7).wait()


def ring(x, dy, gate, up, w_gate, w_up, w_down):
    rows, width = dy.shape
    ff = gate.shape[1]
    chunk, half = rows // 4, width // 2
    piece = jax.ShapeDtypeStruct((chunk, half), BF16)
    dma = pltpu.SemaphoreType.DMA
    return pl.pallas_call(
        ring_kernel,
        name="ring",
        out_shape=(piece,) * 6
        + (jax.ShapeDtypeStruct((rows, ff), BF16),)
        + (jax.ShapeDtypeStruct((width, ff), BF16),) * 2,
        in_specs=[ANY] * 7,
        out_specs=(ANY,) * 9,
        scratch_shapes=[
            pltpu.VMEM((width, ff), BF16),
            pltpu.VMEM((width, ff), BF16),
            pltpu.VMEM((ff, width), BF16),
            pltpu.VMEM((rows, ff), BF16),
            pltpu.VMEM((rows, ff), BF16),
            pltpu.VMEM((2, BLK, width), BF16),
            pltpu.VMEM((2, BLK, ff), BF16),
            pltpu.VMEM((2, BLK, ff), BF16),
            pltpu.VMEM((2, BLK, ff), BF16),
            pltpu.VMEM((12, BLK, half), BF16),
            pltpu.VMEM((12, BLK, half), BF16),
            pltpu.VMEM((2, chunk, half), BF16),
            pltpu.VMEM((2, rows, XT), BF16),
            pltpu.VMEM((2, XT, ff), BF16),
            pltpu.VMEM((2, XT, ff), BF16),
            dma((ff // NT,)),
            dma((2, 2)),
            dma((2, 3)),
            dma((2,)),
            dma((12,)),
            dma((12,)),
            dma((8,)),
            dma((8,)),
            dma((2, 2)),
            dma((2,)),
            dma((2, 2)),
        ],
        compiler_params=pltpu.CompilerParams(collective_id=0, has_side_effects=True, vmem_limit_bytes=60 << 20),
        cost_estimate=pl.CostEstimate(flops=10 * rows * width * ff, bytes_accessed=100 << 20, transcendentals=rows * ff),
    )(x, dy, gate, up, w_gate, w_up, w_down)


def place_copies(pairs, stage, sems):
    return [
        (pltpu.make_async_copy(s, v, sems.at[i, 0]), pltpu.make_async_copy(v, d, sems.at[i, 1]))
        for i, ((s, d), v) in enumerate(zip(pairs, stage))
    ]


def rest_kernel(hid, dy, own_a, own_b, r_a, r_b, l_a, l_b, g_in, u_in, dw_down, dx, g_out, u_out, pieces, gu, sems):
    me = lax.axis_index("tp")
    chunk, half = own_a.shape
    step, last = pl.program_id(0), pl.num_programs(0) - 1
    pairs, stage = [(g_in, g_out), (u_in, u_out)], [gu.at[0], gu.at[1]]
    for k, (a, b) in ((0, (own_a, own_b)), (1, (r_a, r_b)), (3, (l_a, l_b))):
        r = pl.ds(pl.multiple_of(lax.rem(me + k, 4) * chunk, chunk), chunk)
        for h, src in enumerate((a, b)):
            stage.append(pieces.at[len(pairs) - 2])
            pairs.append((src, dx.at[r, pl.ds(h * half, half)]))
    copies = place_copies(pairs, stage, sems)

    @pl.when(step == 0)
    def _():
        for read, _ in copies:
            read.start()

    dw_down[...] = dot(hid[...], dy[...], 0, 0).astype(BF16)

    @pl.when(step == 1)
    def _():
        for read, write in copies:
            read.wait()
            write.start()

    @pl.when(step == last)
    def _():
        for _, write in copies:
            write.wait()


def rest(hid, dy, pieces, dw_gate, dw_up):
    rows, width = dy.shape
    ff = hid.shape[1]
    chunk, half = rows // 4, width // 2
    return pl.pallas_call(
        rest_kernel,
        name="rest",
        grid=(ff // NT,),
        out_shape=(
            jax.ShapeDtypeStruct((ff, width), BF16),
            jax.ShapeDtypeStruct((rows, width), BF16),
            jax.ShapeDtypeStruct(dw_gate.shape, BF16),
            jax.ShapeDtypeStruct(dw_up.shape, BF16),
        ),
        in_specs=[pl.BlockSpec((rows, NT), lambda i: (0, i)), pl.BlockSpec((rows, width), lambda i: (0, 0))] + [ANY] * 8,
        out_specs=(pl.BlockSpec((NT, width), lambda i: (i, 0)), ANY, ANY, ANY),
        scratch_shapes=[
            pltpu.VMEM((6, chunk, half), BF16),
            pltpu.VMEM((2,) + dw_gate.shape, BF16),
            pltpu.SemaphoreType.DMA((8, 2)),
        ],
        compiler_params=pltpu.CompilerParams(vmem_limit_bytes=56 << 20),
        cost_estimate=pl.CostEstimate(flops=2 * rows * width * ff, bytes_accessed=60 << 20, transcendentals=0),
    )(hid, dy, *pieces, dw_gate, dw_up)


def place_kernel(p_a, p_b, dx_in, dx, stage, sems):
    me = lax.axis_index("tp")
    chunk, half = p_a.shape
    r = pl.ds(pl.multiple_of(lax.rem(me + 2, 4) * chunk, chunk), chunk)
    pairs = [(src, dx.at[r, pl.ds(h * half, half)]) for h, src in enumerate((p_a, p_b))]
    copies = place_copies(pairs, [stage.at[0], stage.at[1]], sems)
    for read, _ in copies:
        read.start()
    for read, write in copies:
        read.wait()
        write.start()
    for _, write in copies:
        write.wait()


def place(p_a, p_b, dx):
    return pl.pallas_call(
        place_kernel,
        name="place",
        out_shape=jax.ShapeDtypeStruct(dx.shape, dx.dtype),
        in_specs=[ANY] * 3,
        out_specs=ANY,
        scratch_shapes=[pltpu.VMEM((2,) + p_a.shape, BF16), pltpu.SemaphoreType.DMA((2, 2))],
        input_output_aliases={2: 0},
        compiler_params=pltpu.CompilerParams(vmem_limit_bytes=8 << 20),
    )(p_a, p_b, dx)


def solution(mesh):
    n = mesh.shape["tp"]
    assert n == 4
    to_left = [(i, (i - 1) % n) for i in range(n)]
    to_right = [(i, (i + 1) % n) for i in range(n)]

    def step(x, dy, gate, up, w_gate, w_up, w_down):
        *pieces, hid, dw_gate, dw_up = ring(x, dy, gate, up, w_gate, w_up, w_down)
        p_a = lax.ppermute(pieces[2], "tp", to_left)
        p_b = lax.ppermute(pieces[5], "tp", to_right)
        dw_down, dx, dw_gate, dw_up = rest(hid, dy, pieces, dw_gate, dw_up)
        return place(p_a, p_b, dx), dw_gate, dw_up, dw_down

    tokens, columns, rows = P("dp", None), P(None, "tp"), P("tp", None)
    return jax.shard_map(
        step,
        mesh=mesh,
        in_specs=(tokens, tokens, P("dp", "tp"), P("dp", "tp"), columns, columns, rows),
        out_specs=(tokens, P("dp", "tp"), P("dp", "tp"), P(("dp", "tp"), None)),
        check_vma=False,
    )
```

profile of v0, /device:TPU:112, one launch (start us, length us, event | category | flops | bytes accessed | tf_op | source)
XLA Modules:
  0.0 156.5 jit_solution(12267185476185681335)
XLA Ops:
  0.6 128.0 %ring.1 = (bf16[512,1024]{1,0:T(8,128)(2,1)}, bf16[512,1024]{1,0:T(8,128)(2,1)}, bf16[512,1024]{1,0:T(8,128)(2,1)}, bf16[512,1024]{1,0:T(8,128)(2,1)}, bf16[512,...) custom-call(bf16[2048,2048]{1,0:T(8,128)(2,1)} %x.1, ...), custom_call_target="tpu_custom_call" | custom-call | flops 53687091200 | bytes 104857600 | tf_op jit(solution)/shard_map/ring/pallas_call | solution.py:252
  128.6 0.8 collective-permute-start
  129.4 1.3 collective-permute-start.1
  130.8 22.0 %rest.1 = (bf16[1280,2048]{1,0:T(8,128)(2,1)}, bf16[2048,2048]{1,0:T(8,128)(2,1)}, bf16[2048,1280]{1,0:T(8,128)(2,1)}, bf16[2048,1280]{1,0:T(8,128)(2,1)}) custom-call(bf16[2048,1280]{1,0:T(8,128)(2,1)} %get-tuple-element.19.hid, bf16[2048,2048]{1,0:T(8,128)(2,1)} %dy.3, bf16[512,1024]{1,0:T(8,128)(2,1)} %get-tuple-element.20.own_a, ...), custom_call_target="tpu_custom_call" | custom-call | flops 10737418240 | bytes 62914560 | tf_op jit(solution)/shard_map/rest/pallas_call | solution.py:335
  152.8 0.4 collective-permute-done.p_a
  153.2 1.6 %collective-permute-done.1.p_b = bf16[512,1024]{1,0:T(8,128)(2,1)S(1)} collective-permute-done((bf16[512,1024]{1,0:T(8,128)(2,1)}, bf16[512,1024]{1,0:T(8,128)(2,1)S(1)}, u32[]{:S(2)}, u32[]{:S(2)}) %collective-permute-start.1) | collective-permute-done | bytes 1048608 | tf_op jit(solution)/shard_map/ppermute | solution.py:394
  154.8 1.5 place.1
Async XLA Ops:
  128.6 24.6 %collective-permute-start = (bf16[512,1024]{1,0:T(8,128)(2,1)}, bf16[512,1024]{1,0:T(8,128)(2,1)S(1)}, u32[]{:S(2)}, u32[]{:S(2)}) collective-permute-start(bf16[512,1024]{1,0:T(8,128)(2,1)} %get-tuple-element.17.r_a), channel_id=1, source_target_pairs={{0,3},{1,0},{2,1},{3,2},{4,7},{5,4},{6,5},{7,6},{8,11},{9,8},{10,9... | collective-permute-start | bytes 3145736 | tf_op jit(solution)/shard_map/ppermute | solution.py:393
  129.4 25.4 %collective-permute-start.1 = (bf16[512,1024]{1,0:T(8,128)(2,1)}, bf16[512,1024]{1,0:T(8,128)(2,1)S(1)}, u32[]{:S(2)}, u32[]{:S(2)}) collective-permute-start(bf16[512,1024]{1,0:T(8,128)(2,1)} %get-tuple-element.18.l_b), channel_id=1, source_target_pairs={{0,1},{1,2},{2,3},{3,0},{4,5},{5,6},{6,7},{7,4},{8,9},{9,10},{10,1... | collective-permute-start | bytes 3145736 | tf_op jit(solution)/shard_map/ppermute | solution.py:394
where the time goes:
time: 157 us
  Pallas kernels  152 us (97%)
  starting transfers between devices  2.1 us (1%)
  waiting for transfers between devices  2.04 us (1%)
    pallas_call x1, Pallas kernels, ring(): pl.pallas_call(ring_kernel, name='ring', out_shape=(piece,) * 6 + (jax.Sh...  128 us
    pallas_call x1, Pallas kernels, rest(): pl.pallas_call(rest_kernel, name='rest', grid=(ff // NT,), out_shape=(jax...  22 us
  transfers between devices with their start and end apart: 2, of which 2 were waited for; matrix products, arithmetic and copies ran while one was open for 0% of the time, Pallas kernels for 14%

commit v1 on v0

--- a/solution.py
+++ b/solution.py
@@ -14,7 +14,11 @@
 C = math.sqrt(2.0 / math.pi)
 BLK = 256
 NT = 256
+DT = 512
+AHEAD = 3
 XT = 256
+
+ORDER = ((2, 0), (2, 1), (3, 0), (1, 0), (3, 1), (1, 1), (0, 0), (0, 1))
 
 
 def dot(a, b, ca, cb):
@@ -25,7 +29,7 @@
     x, dy, gate, up, w_gate, w_up, w_down,
     own_a, own_b, r_a, r_b, l_a, l_b, hid, dw_gate, dw_up,
     wg, wu, wd, dg, du, dyb, gb, ub, hidb, snd, rcv, own, xb, og, ou,
-    wd_sem, w_sem, blk_sem, hid_sem, ssem, rsem, ag_ssem, ag_rsem, own_sem, x_sem, o_sem,
+    wd_sem, w_sem, blk_sem, hid_sem, ssem, rsem, head_ssem, head_rsem, ag_ssem, ag_rsem, own_sem, x_sem, o_sem,
 ):
     me = lax.axis_index("tp")
     right, left = lax.rem(me + 1, 4), lax.rem(me + 3, 4)
@@ -33,41 +37,39 @@
     ff = gate.shape[1]
     chunk, half = rows // 4, width // 2
 
-    order = ((2, 0), (2, 1), (3, 0), (1, 0), (3, 1), (1, 1), (0, 0), (0, 1))
-
     def start_row(j):
-        k, b = order[j]
+        k, b = ORDER[j]
         return pl.multiple_of(lax.rem(me + k, 4) * chunk + b * BLK, BLK)
 
     def block_copies(j):
         s, r = j % 2, pl.ds(start_row(j), BLK)
-        return (
+        return [
             pltpu.make_async_copy(dy.at[r], dyb.at[s], blk_sem.at[s, 0]),
             pltpu.make_async_copy(gate.at[r], gb.at[s], blk_sem.at[s, 1]),
             pltpu.make_async_copy(up.at[r], ub.at[s], blk_sem.at[s, 2]),
+        ]
+
+    def span(n, size):
+        return pl.ds(n * size if isinstance(n, int) else pl.multiple_of(n * size, size), size)
+
+    def wd_copy(n):
+        r = span(n, NT)
+        return pltpu.make_async_copy(w_down.at[r], wd.at[r], wd_sem.at[n])
+
+    def w_copies(q):
+        r = span(q, DT)
+        return (
+            pltpu.make_async_copy(w_gate.at[r], wg.at[r], w_sem.at[0, q]),
+            pltpu.make_async_copy(w_up.at[r], wu.at[r], w_sem.at[1, q]),
         )
 
-    def wd_copy(n):
-        r = pl.ds(n * NT, NT)
-        return pltpu.make_async_copy(w_down.at[r], wd.at[r], wd_sem.at[n])
-
-    def w_copy(i, h):
-        r = pl.ds(h * half, half)
-        return pltpu.make_async_copy((w_gate, w_up)[i].at[r], (wg, wu)[i].at[r], w_sem.at[i, h])
-
-    nt = ff // NT
+    def start(copies):
+        for c in copies:
+            c.start()
+
+    nt, per_half = ff // NT, half // DT
     first = block_copies(0)
-    first[0].start()
-    wd_copy(0).start()
-    first[1].start()
-    first[2].start()
-    for n in range(1, nt):
-        wd_copy(n).start()
-    for h in range(2):
-        for i in range(2):
-            w_copy(i, h).start()
-    for c in block_copies(1):
-        c.start()
+    start(first[:1] + [wd_copy(0)] + first[1:] + [wd_copy(n) for n in range(1, AHEAD)])
 
     barrier = pltpu.get_barrier_semaphore()
     for d in (left, right):
@@ -76,73 +78,104 @@
     def hid_copy(j):
         return pltpu.make_async_copy(hidb.at[j % 2], hid.at[pl.ds(start_row(j), BLK)], hid_sem.at[j % 2])
 
+    def backward(j, n, dh):
+        s, r, cols = j % 2, pl.ds(start_row(j), BLK), span(n, NT)
+        g = gb[s, :, cols].astype(F32)
+        u = ub[s, :, cols].astype(F32)
+        g2 = g * g
+        t = jnp.tanh(C * (g + 0.044715 * (g * g2)))
+        cdf = 0.5 * (1.0 + t)
+        act = g * cdf
+        hidb[s, :, cols] = (act * u).astype(BF16)
+        du[r, cols] = (dh * act).astype(BF16)
+        slope = cdf + (0.5 * C) * g * (1.0 - t * t) * (1.0 + (3 * 0.044715) * g2)
+        dg[r, cols] = (dh * u * slope).astype(BF16)
+
+    def hidden_first():
+        for c in first:
+            c.wait()
+
+        @pl.loop(0, nt)
+        def _(n):
+            wd_copy(n).wait()
+
+            @pl.when(n < nt - AHEAD)
+            def _():
+                wd_copy(n + AHEAD).start()
+
+            @pl.when(n >= nt - AHEAD)
+            def _():
+                i = n - (nt - AHEAD)
+                start(w_copies(lax.rem(i, 2) * per_half + i // 2))
+
+            backward(0, n, dot(dyb[0], wd[span(n, NT), :], 1, 1))
+
+        for i in range(AHEAD, 2 * per_half):
+            start(w_copies(i % 2 * per_half + i // 2))
+        start(block_copies(1))
+        hid_copy(0).start()
+
     def hidden(j):
-        s, r0 = j % 2, start_row(j)
+        s = j % 2
         for c in block_copies(j):
             c.wait()
         if j >= 2:
             hid_copy(j - 2).wait()
 
-        def tile(n):
-            cols = pl.ds(pl.multiple_of(n * NT, NT), NT)
-            dh = dot(dyb[s], wd[cols, :], 1, 1)
-            g = gb[s, :, cols].astype(F32)
-            u = ub[s, :, cols].astype(F32)
-            g2 = g * g
-            t = jnp.tanh(C * (g + 0.044715 * (g * g2)))
-            cdf = 0.5 * (1.0 + t)
-            act = g * cdf
-            hidb[s, :, cols] = (act * u).astype(BF16)
-            du[pl.ds(r0, BLK), cols] = (dh * act).astype(BF16)
-            slope = cdf + (0.5 * C) * g * (1.0 - t * t) * (1.0 + (3 * 0.044715) * g2)
-            dg[pl.ds(r0, BLK), cols] = (dh * u * slope).astype(BF16)
-
-        if j == 0:
-            for n in range(nt):
-                wd_copy(n).wait()
-                tile(n)
-        else:
-            pl.loop(0, nt)(tile)
-        if j + 2 < len(order):
+        @pl.loop(0, nt)
+        def _(n):
+            backward(j, n, dot(dyb[s], wd[span(n, NT), :], 1, 1))
+
+        if j < len(ORDER) - 2:
             for c in block_copies(j + 2):
                 c.start()
         hid_copy(j).start()
 
+    def columns(j, q, adds, dst, rows_, cols):
+        r, wr = pl.ds(start_row(j), BLK), span(q, DT)
+        t = dot(dg[r, :], wg[wr, :], 1, 1) + dot(du[r, :], wu[wr, :], 1, 1)
+        for a in adds:
+            t = t + rcv[a, :, cols].astype(F32)
+        dst[rows_, cols] = t.astype(BF16)
+
     def term(j, h, adds, dst, row):
-        r = pl.ds(start_row(j), BLK)
-        if j == 0:
-            w_copy(0, h).wait()
-            w_copy(1, h).wait()
-
-        @pl.loop(0, half // 512)
+        @pl.loop(0, per_half)
         def _(i):
-            wr = pl.ds(pl.multiple_of(h * half + i * 512, 512), 512)
-            cols = pl.ds(pl.multiple_of(i * 512, 512), 512)
-            t = dot(dg[r, :], wg[wr, :], 1, 1) + dot(du[r, :], wu[wr, :], 1, 1)
-            for a in adds:
-                t = t + rcv[a, :, cols].astype(F32)
-            dst[row : row + BLK, cols] = t.astype(BF16)
+            columns(j, h * per_half + i, adds, dst, pl.ds(row, BLK), span(i, DT))
 
     def slot(kind, b):
         return kind * 2 + b
 
-    def reduce_copy(kind, b):
+    def reduce_copy(kind, b, rect=None):
         s = slot(kind, b)
+        src, dst, sems = snd.at[s], rcv.at[s], (ssem.at[s], rsem.at[s])
+        if rect is not None:
+            src, dst = src.at[:, span(rect, DT)], dst.at[:, span(rect, DT)]
+            sems = (head_ssem.at[kind // 3, rect], head_rsem.at[kind // 3, rect])
         return pltpu.make_async_remote_copy(
-            src_ref=snd.at[s], dst_ref=rcv.at[s], send_sem=ssem.at[s], recv_sem=rsem.at[s],
+            src_ref=src, dst_ref=dst, send_sem=sems[0], recv_sem=sems[1],
             device_id={"tp": left if kind < 3 else right}, device_id_type=MESH,
         )
 
     def send(j, h, kind, adds=()):
-        b = order[j][1]
+        b = ORDER[j][1]
         term(j, h, adds, snd.at[slot(kind, b)], 0)
         reduce_copy(kind, b).start()
 
-    hidden(0)
-    term(0, 0, (), snd.at[slot(0, 0)], 0)
+    head = range(per_half)
+    hidden_first()
     pl.semaphore_wait(barrier, 2)
-    reduce_copy(0, 0).start()
-    send(0, 1, 3)
+
+    @pl.loop(0, per_half)
+    def _(i):
+        for h, kind in ((0, 0), (1, 3)):
+            q = h * per_half + i
+            for c in w_copies(q):
+                c.wait()
+            columns(0, q, (), snd.at[slot(kind, 0)], pl.ds(0, BLK), span(i, DT))
+            reduce_copy(kind, 0, i).start()
+
+    start(block_copies(2))
     hidden(1)
     send(1, 0, 0)
     send(1, 1, 3)
@@ -150,10 +183,10 @@
         hidden(j)
         send(j, h, kind)
     for b in range(2):
-        reduce_copy(0, b).wait_recv()
-        send(2 + 2 * b, 0, 2, (slot(0, b),))
-        reduce_copy(3, b).wait_recv()
-        send(3 + 2 * b, 1, 5, (slot(3, b),))
+        for kind, j, h in ((0, 2, 0), (3, 3, 1)):
+            for i in head if b == 0 else (None,):
+                reduce_copy(kind, b, i).wait_recv()
+            send(j + 2 * b, h, kind + 2, (slot(kind, b),))
     hidden(6)
     hidden(7)
 
@@ -233,7 +266,8 @@
 
     for kind in range(6):
         for b in range(2):
-            reduce_copy(kind, b).wait_send()
+            for i in head if kind % 3 == 0 and b == 0 else (None,):
+                reduce_copy(kind, b, i).wait_send()
     for b in range(2):
         for c in gather_copies(b):
             c.wait()
@@ -274,11 +308,13 @@
             pltpu.VMEM((2, XT, ff), BF16),
             pltpu.VMEM((2, XT, ff), BF16),
             dma((ff // NT,)),
-            dma((2, 2)),
+            dma((2, width // DT)),
             dma((2, 3)),
             dma((2,)),
             dma((12,)),
             dma((12,)),
+            dma((2, half // DT)),
+            dma((2, half // DT)),
             dma((8,)),
             dma((8,)),
             dma((2, 2)),

time: 157 us -> 154 us (0.981)
  Pallas kernels: 152 us -> 149 us
    pallas_call x1, Pallas kernels: 128 us -> 125 us  [ring(): pl.pallas_call(ring_kernel, name='ring', out_shape=(piece,) * 6 + (jax.Sh...]
where the time goes in v1:
time: 154 us
  Pallas kernels  149 us (97%)
  starting transfers between devices  2.1 us (1%)
  waiting for transfers between devices  2.06 us (1%)
    pallas_call x1, Pallas kernels, ring(): pl.pallas_call(ring_kernel, name='ring', out_shape=(piece,) * 6 + (jax.Sh...  125 us
    pallas_call x1, Pallas kernels, rest(): pl.pallas_call(rest_kernel, name='rest', grid=(ff // NT,), out_shape=(jax...  22 us
  transfers between devices with their start and end apart: 2, of which 2 were waited for; matrix products, arithmetic and copies ran while one was open for 0% of the time, Pallas kernels for 14%

profile of v1, /device:TPU:112, one launch (start us, length us, event | category | flops | bytes accessed | tf_op | source)
XLA Modules:
  0.0 153.6 jit_solution(17958390922266315295)
XLA Ops:
  0.6 125.1 %ring.1 = (bf16[512,1024]{1,0:T(8,128)(2,1)}, bf16[512,1024]{1,0:T(8,128)(2,1)}, bf16[512,1024]{1,0:T(8,128)(2,1)}, bf16[512,1024]{1,0:T(8,128)(2,1)}, bf16[512,...) custom-call(bf16[2048,2048]{1,0:T(8,128)(2,1)} %x.1, ...), custom_call_target="tpu_custom_call" | custom-call | flops 53687091200 | bytes 104857600 | tf_op jit(solution)/shard_map/ring/pallas_call | solution.py:286
  125.7 0.8 collective-permute-start
  126.5 1.3 collective-permute-start.1
  127.8 22.0 %rest.1 = (bf16[1280,2048]{1,0:T(8,128)(2,1)}, bf16[2048,2048]{1,0:T(8,128)(2,1)}, bf16[2048,1280]{1,0:T(8,128)(2,1)}, bf16[2048,1280]{1,0:T(8,128)(2,1)}) custom-call(bf16[2048,1280]{1,0:T(8,128)(2,1)} %get-tuple-element.19.hid, bf16[2048,2048]{1,0:T(8,128)(2,1)} %dy.3, bf16[512,1024]{1,0:T(8,128)(2,1)} %get-tuple-element.20.own_a, ...), custom_call_target="tpu_custom_call" | custom-call | flops 10737418240 | bytes 62914560 | tf_op jit(solution)/shard_map/rest/pallas_call | solution.py:371
  149.8 0.4 collective-permute-done.p_a
  150.3 1.6 %collective-permute-done.1.p_b = bf16[512,1024]{1,0:T(8,128)(2,1)S(1)} collective-permute-done((bf16[512,1024]{1,0:T(8,128)(2,1)}, bf16[512,1024]{1,0:T(8,128)(2,1)S(1)}, u32[]{:S(2)}, u32[]{:S(2)}) %collective-permute-start.1) | collective-permute-done | bytes 1048608 | tf_op jit(solution)/shard_map/ppermute | solution.py:430
  151.9 1.5 place.1
Async XLA Ops:
  125.7 24.6 %collective-permute-start = (bf16[512,1024]{1,0:T(8,128)(2,1)}, bf16[512,1024]{1,0:T(8,128)(2,1)S(1)}, u32[]{:S(2)}, u32[]{:S(2)}) collective-permute-start(bf16[512,1024]{1,0:T(8,128)(2,1)} %get-tuple-element.17.r_a), channel_id=1, source_target_pairs={{0,3},{1,0},{2,1},{3,2},{4,7},{5,4},{6,5},{7,6},{8,11},{9,8},{10,9... | collective-permute-start | bytes 3145736 | tf_op jit(solution)/shard_map/ppermute | solution.py:429
  126.5 25.4 %collective-permute-start.1 = (bf16[512,1024]{1,0:T(8,128)(2,1)}, bf16[512,1024]{1,0:T(8,128)(2,1)S(1)}, u32[]{:S(2)}, u32[]{:S(2)}) collective-permute-start(bf16[512,1024]{1,0:T(8,128)(2,1)} %get-tuple-element.18.l_b), channel_id=1, source_target_pairs={{0,1},{1,2},{2,3},{3,0},{4,5},{5,6},{6,7},{7,4},{8,9},{9,10},{10,1... | collective-permute-start | bytes 3145736 | tf_op jit(solution)/shard_map/ppermute | solution.py:430

commit v2 on v1

--- a/solution.py
+++ b/solution.py
@@ -15,6 +15,11 @@
 BLK = 256
 NT = 256
 DT = 512
+LATE = 6500
+PARTS = 4
+DEPTH = 18
+RING_VMEM, REST_VMEM = 60, 56
+QUICK = (1, 2)
 AHEAD = 3
 XT = 256
 
@@ -27,9 +32,9 @@
 
 def ring_kernel(
     x, dy, gate, up, w_gate, w_up, w_down,
-    own_a, own_b, r_a, r_b, l_a, l_b, hid, dw_gate, dw_up,
+    own_a, own_b, r_a, r_b, l_a, l_b, hid, dw_gate, dw_up, dw_down,
     wg, wu, wd, dg, du, dyb, gb, ub, hidb, snd, rcv, own, xb, og, ou,
-    wd_sem, w_sem, blk_sem, hid_sem, ssem, rsem, head_ssem, head_rsem, ag_ssem, ag_rsem, own_sem, x_sem, o_sem,
+    wd_sem, w_sem, blk_sem, hid_sem, ssem, rsem, part_sem, head_ssem, head_rsem, ag_ssem, ag_rsem, own_sem, x_sem, o_sem, dy_sem,
 ):
     me = lax.axis_index("tp")
     right, left = lax.rem(me + 1, 4), lax.rem(me + 3, 4)
@@ -68,8 +73,13 @@
             c.start()
 
     nt, per_half = ff // NT, half // DT
-    first = block_copies(0)
-    start(first[:1] + [wd_copy(0)] + first[1:] + [wd_copy(n) for n in range(1, AHEAD)])
+    r0 = pl.ds(start_row(0), BLK)
+    parts = [
+        [pltpu.make_async_copy(a.at[r0, c], b.at[0, :, c], part_sem.at[i, k]) for i, (a, b) in enumerate(((gate, gb), (up, ub)))]
+        for k, c in enumerate((pl.ds(0, NT), pl.ds(NT, ff - NT)))
+    ]
+    first = pltpu.make_async_copy(dy.at[r0], dyb.at[0], blk_sem.at[0, 0])
+    start(parts[0] + [first, wd_copy(0)])
 
     barrier = pltpu.get_barrier_semaphore()
     for d in (left, right):
@@ -79,7 +89,7 @@
         return pltpu.make_async_copy(hidb.at[j % 2], hid.at[pl.ds(start_row(j), BLK)], hid_sem.at[j % 2])
 
     def backward(j, n, dh):
-        s, r, cols = j % 2, pl.ds(start_row(j), BLK), span(n, NT)
+        s, r, cols = j % 2, pl.ds(start_row(j), BLK), pl.ds(0, ff) if n is None else span(n, NT)
         g = gb[s, :, cols].astype(F32)
         u = ub[s, :, cols].astype(F32)
         g2 = g * g
@@ -92,12 +102,19 @@
         dg[r, cols] = (dh * u * slope).astype(BF16)
 
     def hidden_first():
-        for c in first:
+        for c in parts[0]:
             c.wait()
+        start([wd_copy(n) for n in range(1, AHEAD)] + parts[1])
+        first.wait()
 
         @pl.loop(0, nt)
         def _(n):
             wd_copy(n).wait()
+
+            @pl.when(n == 1)
+            def _():
+                for c in parts[1]:
+                    c.wait()
 
             @pl.when(n < nt - AHEAD)
             def _():
@@ -122,26 +139,34 @@
         if j >= 2:
             hid_copy(j - 2).wait()
 
-        @pl.loop(0, nt)
-        def _(n):
-            backward(j, n, dot(dyb[s], wd[span(n, NT), :], 1, 1))
+        if j in QUICK:
+            backward(j, None, dot(dyb[s], wd[...], 1, 1))
+        else:
+
+            @pl.loop(0, nt)
+            def _(n):
+                backward(j, n, dot(dyb[s], wd[span(n, NT), :], 1, 1))
 
         if j < len(ORDER) - 2:
             for c in block_copies(j + 2):
                 c.start()
         hid_copy(j).start()
 
-    def columns(j, q, adds, dst, rows_, cols):
-        r, wr = pl.ds(start_row(j), BLK), span(q, DT)
+    def columns(j, wr, adds, dst, rows_, cols):
+        r = pl.ds(start_row(j), BLK)
         t = dot(dg[r, :], wg[wr, :], 1, 1) + dot(du[r, :], wu[wr, :], 1, 1)
         for a in adds:
             t = t + rcv[a, :, cols].astype(F32)
         dst[rows_, cols] = t.astype(BF16)
 
     def term(j, h, adds, dst, row):
+        if j in QUICK:
+            columns(j, pl.ds(h * half, half), adds, dst, pl.ds(row, BLK), pl.ds(0, half))
+            return
+
         @pl.loop(0, per_half)
         def _(i):
-            columns(j, h * per_half + i, adds, dst, pl.ds(row, BLK), span(i, DT))
+            columns(j, span(h * per_half + i, DT), adds, dst, pl.ds(row, BLK), span(i, DT))
 
     def slot(kind, b):
         return kind * 2 + b
@@ -162,17 +187,21 @@
         term(j, h, adds, snd.at[slot(kind, b)], 0)
         reduce_copy(kind, b).start()
 
-    head = range(per_half)
+    heads = half // DT
+    head = range(heads)
     hidden_first()
     pl.semaphore_wait(barrier, 2)
 
-    @pl.loop(0, per_half)
+    @pl.when(lax.rem(lax.axis_index("dp"), 2) == 0)
+    def _():
+        pl.delay(LATE)
+
+    @pl.loop(0, heads)
     def _(i):
         for h, kind in ((0, 0), (1, 3)):
-            q = h * per_half + i
-            for c in w_copies(q):
+            for c in w_copies(h * per_half + i):
                 c.wait()
-            columns(0, q, (), snd.at[slot(kind, 0)], pl.ds(0, BLK), span(i, DT))
+            columns(0, span(h * heads + i, DT), (), snd.at[slot(kind, 0)], pl.ds(0, BLK), span(i, DT))
             reduce_copy(kind, 0, i).start()
 
     start(block_copies(2))
@@ -231,6 +260,48 @@
             for c in o_copies(hi - 2 + s, s):
                 c.wait()
 
+    dy_halves = (wg.at[:, pl.ds(0, half)], wu.at[:, pl.ds(0, half)])
+    dy_copies = [pltpu.make_async_copy(dy.at[:, pl.ds(h * half, half)], v, dy_sem.at[h]) for h, v in enumerate(dy_halves)]
+
+    def down():
+        def load(i, s):
+            return pltpu.make_async_copy(hid.at[:, span(i, XT)], xb.at[s], x_sem.at[s])
+
+        def save(i, s):
+            r = span(i, XT)
+            return (
+                pltpu.make_async_copy(og.at[s, :, pl.ds(0, half)], dw_down.at[r, pl.ds(0, half)], o_sem.at[s, 0]),
+                pltpu.make_async_copy(ou.at[s, :, pl.ds(0, half)], dw_down.at[r, pl.ds(half, half)], o_sem.at[s, 1]),
+            )
+
+        load(0, 0).start()
+        load(1, 1).start()
+        for c in dy_copies:
+            c.wait()
+
+        @pl.loop(0, nt)
+        def _(i):
+            s = lax.rem(i, 2)
+            load(i, s).wait()
+
+            @pl.when(i >= 2)
+            def _():
+                for c in save(i, s):
+                    c.wait()
+
+            og[s, :, :half] = dot(xb[s], wg[:, :half], 0, 0).astype(BF16)
+            ou[s, :, :half] = dot(xb[s], wu[:, :half], 0, 0).astype(BF16)
+
+            @pl.when(i + 2 < nt)
+            def _():
+                load(i + 2, s).start()
+
+            start(save(i, s))
+
+        for i in (nt - 2, nt - 1):
+            for c in save(i, i % 2):
+                c.wait()
+
     def gather_copies(b):
         r = pl.ds(b * BLK, BLK)
         for d, h, dst in ((left, 0, r_a), (right, 1, l_b), (left, 1, r_b), (right, 0, l_a)):
@@ -262,7 +333,11 @@
     weights(0, steps // 2)
     finish(0)
     finish(1)
+    start(dy_copies)
+    hid_copy(6).wait()
+    hid_copy(7).wait()
     weights(steps // 2, steps)
+    down()
 
     for kind in range(6):
         for b in range(2):
@@ -273,14 +348,13 @@
             c.wait()
         for c in own_copies(b):
             c.wait()
-    hid_copy(6).wait()
-    hid_copy(7).wait()
 
 
 def ring(x, dy, gate, up, w_gate, w_up, w_down):
     rows, width = dy.shape
     ff = gate.shape[1]
     chunk, half = rows // 4, width // 2
+    assert rows == width and half <= ff
     piece = jax.ShapeDtypeStruct((chunk, half), BF16)
     dma = pltpu.SemaphoreType.DMA
     return pl.pallas_call(
@@ -288,9 +362,10 @@
         name="ring",
         out_shape=(piece,) * 6
         + (jax.ShapeDtypeStruct((rows, ff), BF16),)
-        + (jax.ShapeDtypeStruct((width, ff), BF16),) * 2,
+        + (jax.ShapeDtypeStruct((width, ff), BF16),) * 2
+        + (jax.ShapeDtypeStruct((ff, width), BF16),),
         in_specs=[ANY] * 7,
-        out_specs=(ANY,) * 9,
+        out_specs=(ANY,) * 10,
         scratch_shapes=[
             pltpu.VMEM((width, ff), BF16),
             pltpu.VMEM((width, ff), BF16),
@@ -313,6 +388,7 @@
             dma((2,)),
             dma((12,)),
             dma((12,)),
+            dma((2, 2)),
             dma((2, half // DT)),
             dma((2, half // DT)),
             dma((8,)),
@@ -320,9 +396,10 @@
             dma((2, 2)),
             dma((2,)),
             dma((2, 2)),
+            dma((2,)),
         ],
-        compiler_params=pltpu.CompilerParams(collective_id=0, has_side_effects=True, vmem_limit_bytes=60 << 20),
-        cost_estimate=pl.CostEstimate(flops=10 * rows * width * ff, bytes_accessed=100 << 20, transcendentals=rows * ff),
+        compiler_params=pltpu.CompilerParams(collective_id=0, has_side_effects=True, vmem_limit_bytes=RING_VMEM << 20),
+        cost_estimate=pl.CostEstimate(flops=12 * rows * width * ff, bytes_accessed=100 << 20, transcendentals=rows * ff),
     )(x, dy, gate, up, w_gate, w_up, w_down)
 
 
@@ -333,61 +410,53 @@
     ]
 
 
-def rest_kernel(hid, dy, own_a, own_b, r_a, r_b, l_a, l_b, g_in, u_in, dw_down, dx, g_out, u_out, pieces, gu, sems):
+def rest_kernel(own_a, own_b, r_a, r_b, l_a, l_b, g_in, u_in, d_in, dx, g_out, u_out, d_out, pieces, gu, dn, sems):
     me = lax.axis_index("tp")
     chunk, half = own_a.shape
-    step, last = pl.program_id(0), pl.num_programs(0) - 1
-    pairs, stage = [(g_in, g_out), (u_in, u_out)], [gu.at[0], gu.at[1]]
+    pairs, stage = [], []
     for k, (a, b) in ((0, (own_a, own_b)), (1, (r_a, r_b)), (3, (l_a, l_b))):
         r = pl.ds(pl.multiple_of(lax.rem(me + k, 4) * chunk, chunk), chunk)
         for h, src in enumerate((a, b)):
-            stage.append(pieces.at[len(pairs) - 2])
+            stage.append(pieces.at[len(pairs)])
             pairs.append((src, dx.at[r, pl.ds(h * half, half)]))
+    for src, dst, v in ((g_in, g_out, gu.at[0]), (u_in, u_out, gu.at[1]), (d_in, d_out, dn)):
+        n = src.shape[0] // PARTS
+        for i in range(PARTS):
+            r = pl.ds(i * n, n)
+            pairs.append((src.at[r], dst.at[r]))
+            stage.append(v.at[r])
     copies = place_copies(pairs, stage, sems)
-
-    @pl.when(step == 0)
-    def _():
-        for read, _ in copies:
-            read.start()
-
-    dw_down[...] = dot(hid[...], dy[...], 0, 0).astype(BF16)
-
-    @pl.when(step == 1)
-    def _():
-        for read, write in copies:
-            read.wait()
-            write.start()
-
-    @pl.when(step == last)
-    def _():
-        for _, write in copies:
-            write.wait()
-
-
-def rest(hid, dy, pieces, dw_gate, dw_up):
-    rows, width = dy.shape
-    ff = hid.shape[1]
-    chunk, half = rows // 4, width // 2
+    for read, _ in copies[:DEPTH]:
+        read.start()
+    for i, (read, write) in enumerate(copies):
+        read.wait()
+        write.start()
+        if i + DEPTH < len(copies):
+            copies[i + DEPTH][0].start()
+    for _, write in copies:
+        write.wait()
+
+
+def rest(pieces, dw_gate, dw_up, dw_down):
+    chunk, half = pieces[0].shape
+    grads = (dw_gate, dw_up, dw_down)
+    dx = jax.ShapeDtypeStruct((4 * chunk, 2 * half), BF16)
+    moved = 6 * pieces[0].size + 3 * dw_gate.size
     return pl.pallas_call(
         rest_kernel,
         name="rest",
-        grid=(ff // NT,),
-        out_shape=(
-            jax.ShapeDtypeStruct((ff, width), BF16),
-            jax.ShapeDtypeStruct((rows, width), BF16),
-            jax.ShapeDtypeStruct(dw_gate.shape, BF16),
-            jax.ShapeDtypeStruct(dw_up.shape, BF16),
-        ),
-        in_specs=[pl.BlockSpec((rows, NT), lambda i: (0, i)), pl.BlockSpec((rows, width), lambda i: (0, 0))] + [ANY] * 8,
-        out_specs=(pl.BlockSpec((NT, width), lambda i: (i, 0)), ANY, ANY, ANY),
+        out_shape=(dx, *(jax.ShapeDtypeStruct(g.shape, BF16) for g in grads)),
+        in_specs=[ANY] * 9,
+        out_specs=(ANY,) * 4,
         scratch_shapes=[
             pltpu.VMEM((6, chunk, half), BF16),
             pltpu.VMEM((2,) + dw_gate.shape, BF16),
-            pltpu.SemaphoreType.DMA((8, 2)),
+            pltpu.VMEM(dw_down.shape, BF16),
+            pltpu.SemaphoreType.DMA((6 + 3 * PARTS, 2)),
         ],
-        compiler_params=pltpu.CompilerParams(vmem_limit_bytes=56 << 20),
-        cost_estimate=pl.CostEstimate(flops=2 * rows * width * ff, bytes_accessed=60 << 20, transcendentals=0),
-    )(hid, dy, *pieces, dw_gate, dw_up)
+        compiler_params=pltpu.CompilerParams(vmem_limit_bytes=REST_VMEM << 20),
+        cost_estimate=pl.CostEstimate(flops=12_000_000_000, bytes_accessed=4 * moved, transcendentals=0),
+    )(*pieces, *grads)
 
 
 def place_kernel(p_a, p_b, dx_in, dx, stage, sems):
@@ -425,11 +494,11 @@
     to_right = [(i, (i + 1) % n) for i in range(n)]
 
     def step(x, dy, gate, up, w_gate, w_up, w_down):
-        *pieces, hid, dw_gate, dw_up = ring(x, dy, gate, up, w_gate, w_up, w_down)
+        *pieces, _, dw_gate, dw_up, dw_down = ring(x, dy, gate, up, w_gate, w_up, w_down)
         p_a = lax.ppermute(pieces[2], "tp", to_left)
         p_b = lax.ppermute(pieces[5], "tp", to_right)
-        dw_down, dx, dw_gate, dw_up = rest(hid, dy, pieces, dw_gate, dw_up)
-        return place(p_a, p_b, dx), dw_gate, dw_up, dw_down
+        dx, *grads = rest(pieces, dw_gate, dw_up, dw_down)
+        return place(p_a, p_b, dx), *grads
 
     tokens, columns, rows = P("dp", None), P(None, "tp"), P("tp", None)
     return jax.shard_map(

time: 154 us -> 152 us (0.987)
  Pallas kernels: 149 us -> 143 us
  waiting for transfers between devices: 2.06 us -> 5.81 us
    pallas_call x1, Pallas kernels: 22 us -> 15.4 us  [rest(): pl.pallas_call(rest_kernel, name='rest', out_shape=(dx, *(jax.ShapeDtypeS...]
    ppermute x1, waiting for transfers between devices: 0.44 us -> 4.18 us  [step(): p_a = lax.ppermute(pieces[2], 'tp', to_left)]
  transfers between devices with their start and end apart: 2 -> 2, of which waited for: 2 -> 2; matrix products, arithmetic and copies ran while one was open for 0% -> 0% of each run, Pallas kernels for 14% -> 10%
where the time goes in v2:
time: 152 us
  Pallas kernels  143 us (94%)
  waiting for transfers between devices  5.81 us (4%)
  starting transfers between devices  2.1 us (1%)
    pallas_call x1, Pallas kernels, ring(): pl.pallas_call(ring_kernel, name='ring', out_shape=(piece,) * 6 + (jax.Sh...  126 us
    pallas_call x1, Pallas kernels, rest(): pl.pallas_call(rest_kernel, name='rest', out_shape=(dx, *(jax.ShapeDtypeS...  15.4 us
    ppermute x1, waiting for transfers between devices, step(): p_a = lax.ppermute(pieces[2], 'tp', to_left)  4.18 us
  transfers between devices with their start and end apart: 2, of which 2 were waited for; matrix products, arithmetic and copies ran while one was open for 0% of the time, Pallas kernels for 10%

profile of v2, /device:TPU:112, one launch (start us, length us, event | category | flops | bytes accessed | tf_op | source)
XLA Modules:
  0.0 152.0 jit_solution(4339481523321299938)
XLA Ops:
  0.6 126.4 %ring.1 = (bf16[512,1024]{1,0:T(8,128)(2,1)}, bf16[512,1024]{1,0:T(8,128)(2,1)}, bf16[512,1024]{1,0:T(8,128)(2,1)}, bf16[512,1024]{1,0:T(8,128)(2,1)}, bf16[512,...) custom-call(bf16[2048,2048]{1,0:T(8,128)(2,1)} %x.1, ...), custom_call_target="tpu_custom_call" | custom-call | flops 64424509440 | bytes 104857600 | tf_op jit(solution)/shard_map/ring/pallas_call | solution.py:360
  127.0 0.8 collective-permute-start
  127.8 1.3 collective-permute-start.1
  129.1 15.4 %rest.1 = (bf16[2048,2048]{1,0:T(8,128)(2,1)}, bf16[2048,1280]{1,0:T(8,128)(2,1)}, bf16[2048,1280]{1,0:T(8,128)(2,1)}, bf16[1280,2048]{1,0:T(8,128)(2,1)}) custom-call(bf16[512,1024]{1,0:T(8,128)(2,1)} %get-tuple-element.19.own_a, bf16[512,1024]{1,0:T(8,128)(2,1)} %get-tuple-element.20.own_b, bf16[512,1024]{1,0:T(8,128)(2,1)} %get-tuple-element.17.r_a, ...), custom_call_target="tpu_custom_call" | custom-call | flops 12000000000 | bytes 44040192 | tf_op jit(solution)/shard_map/rest/pallas_call | solution.py:445
  144.5 4.2 %collective-permute-done.p_a = bf16[512,1024]{1,0:T(8,128)(2,1)S(1)} collective-permute-done((bf16[512,1024]{1,0:T(8,128)(2,1)}, bf16[512,1024]{1,0:T(8,128)(2,1)S(1)}, u32[]{:S(2)}, u32[]{:S(2)}) %collective-permute-start) | collective-permute-done | bytes 1048608 | tf_op jit(solution)/shard_map/ppermute | solution.py:498
  148.7 1.6 %collective-permute-done.1.p_b = bf16[512,1024]{1,0:T(8,128)(2,1)S(1)} collective-permute-done((bf16[512,1024]{1,0:T(8,128)(2,1)}, bf16[512,1024]{1,0:T(8,128)(2,1)S(1)}, u32[]{:S(2)}, u32[]{:S(2)}) %collective-permute-start.1) | collective-permute-done | bytes 1048608 | tf_op jit(solution)/shard_map/ppermute | solution.py:499
  150.3 1.5 place.1
Async XLA Ops:
  127.0 21.7 %collective-permute-start = (bf16[512,1024]{1,0:T(8,128)(2,1)}, bf16[512,1024]{1,0:T(8,128)(2,1)S(1)}, u32[]{:S(2)}, u32[]{:S(2)}) collective-permute-start(bf16[512,1024]{1,0:T(8,128)(2,1)} %get-tuple-element.17.r_a), channel_id=1, source_target_pairs={{0,3},{1,0},{2,1},{3,2},{4,7},{5,4},{6,5},{7,6},{8,11},{9,8},{10,9... | collective-permute-start | bytes 3145736 | tf_op jit(solution)/shard_map/ppermute | solution.py:498
  127.8 22.5 %collective-permute-start.1 = (bf16[512,1024]{1,0:T(8,128)(2,1)}, bf16[512,1024]{1,0:T(8,128)(2,1)S(1)}, u32[]{:S(2)}, u32[]{:S(2)}) collective-permute-start(bf16[512,1024]{1,0:T(8,128)(2,1)} %get-tuple-element.18.l_b), channel_id=1, source_target_pairs={{0,1},{1,2},{2,3},{3,0},{4,5},{5,6},{6,7},{7,4},{8,9},{9,10},{10,1... | collective-permute-start | bytes 3145736 | tf_op jit(solution)/shard_map/ppermute | solution.py:499
